TPU v7x, 128 devices: a whole 4x4x4 slice. The times are simulated.
128 devices in a mesh: gx: 8 (over z_hi, y), gz: 16 (over z_lo, x, core).
Axes of the slice: x: 4, y: 4, z: 4 (z_hi: 2, z_lo: 2; z = z_hi * 2 + z_lo), core: 2. Of those that a mesh axis runs over, the one named last changes fastest.
Arguments:
- high_u: bfloat16 [256, 512, 512], P('gx', 'gz'), may hold values from -6 to 6
- high_v: bfloat16 [256, 512, 512], P('gx', 'gz'), may hold values from -6 to 6
- low_u: bfloat16 [2048, 512], P(('gx', 'gz')), may hold values from -0.25 to 0.25
- low_v: bfloat16 [2048, 512], P(('gx', 'gz')), may hold values from -0.25 to 0.25
- low_kx: int32 [2048], P(('gx', 'gz')), may hold values from 0 to 64, as said below
- low_kz: int32 [2048], P(('gx', 'gz')), may hold values from 0 to 64, as said below
- tau_inverse: bfloat16 [2048, 512, 512], P(('gx', 'gz')), may hold values from -0.25 to 0.25
Outputs:
- high_term: bfloat16 [256, 512, 512], P('gx', 'gz')
- low_response: float32 [2048, 512], P(('gx', 'gz'))
Inputs may be any that keep to these rules, and one draw needn't show every extreme that they name: Slot m holds the retained mode (low_kx[m], low_kz[m]); no two slots hold the same pair; the device that holds slot m owns that mode. `low_kz`: paired with low_kx slot by slot.
All inputs are finite; a program needn't handle non-finite values.
Results may differ from a plain program's by a relative error of at most 0.0047.
Values may be sent and summed in bfloat16 or wider, within the bound.
No kernel may reach another device: no remote copies, remote signals or barrier semaphores. Data moves between devices by JAX's collectives and lax.ppermute only.
A program may use at most 128 MiB of HBM per device.

v0:
```python
import math
import jax
import jax.numpy as jnp
from jax import lax
from jax.sharding import PartitionSpec as P

KL = 32
CONTRACT_FIRST = (((0,), (0,)), ((), ()))


def in_one_piece(arrays, axis, dim, along):
    columns = [a.reshape(*a.shape[:along], -1) for a in arrays]
    both = jnp.concatenate(columns, axis=along)
    whole, at, done = (lax.all_gather(both, axis, axis=dim, tiled=True), 0, [])
    for a, column in zip(arrays, columns):
        section = whole[..., at : at + column.shape[along]]
        done.append(section.reshape(*section.shape[:along], *a.shape[along:]))
        at += column.shape[along]
    return tuple(done)


def cut_along(x, dim, count):
    shape = x.shape
    pieces = x.reshape(*shape[:dim], count, shape[dim] // count, *shape[dim + 1 :])
    return jnp.moveaxis(pieces, dim, 0)


def sent_and_summed(x, axis, dim):
    count = lax.axis_size(axis)
    pieces = lax.all_to_all(cut_along(x, dim, count), axis, 0, 0, tiled=True)
    return jnp.sum(pieces, axis=0)


def axis_table(index, positions, length):
    wavenum = jnp.where(index <= KL, index, index - KL)
    phases = wavenum[:, None] * positions[None, :] % length
    angles = phases.astype(jnp.float32) * (2.0 * math.pi / length)
    return jnp.where((index <= KL)[:, None], jnp.cos(angles), jnp.sin(angles))


def mode_weight(index_x, index_z):
    return jnp.where(index_x > 0, 2.0, 1.0).astype(jnp.float32) * jnp.where(
        index_z > 0, 2.0, 1.0
    ).astype(jnp.float32)


def on_device(high_u, high_v, low_u, low_v, low_kx, low_kz, tau_inverse):
    cells_x, cells_z, levels = high_u.shape
    owned_modes = low_u.shape[0]
    groups_x = lax.axis_size("gx")
    groups_z = lax.axis_size("gz")
    length_x = groups_x * cells_x
    length_z = groups_z * cells_z
    points = cells_x * cells_z
    unitary = 1.0 / math.sqrt(length_x * length_z)
    where_x = lax.axis_index("gx") * cells_x + jnp.arange(cells_x, dtype=jnp.int32)
    where_z = lax.axis_index("gz") * cells_z + jnp.arange(cells_z, dtype=jnp.int32)

    def patterns(index_x, index_z):
        table_x = axis_table(index_x, where_x, length_x)
        table_z = axis_table(index_z, where_z, length_z)
        return (
            (table_x[:, :, None] * table_z[:, None, :])
            .reshape(index_x.shape[0], points)
            .astype(jnp.bfloat16)
        )

    shard_u, shard_v, shard_x, shard_z = in_one_piece(
        (low_u, low_v, low_kx.astype(jnp.bfloat16), low_kz.astype(jnp.bfloat16)), ("gx", "gz"), 0, 1
    )
    index_x = shard_x.astype(jnp.int32)
    index_z = shard_z.astype(jnp.int32)
    stacked = jnp.concatenate([shard_u, shard_v], axis=1)
    coarse = lax.dot_general(
        patterns(index_x, index_z), stacked, CONTRACT_FIRST, preferred_element_type=jnp.float32
    )
    add_every_x = index_x
    add_every_z = index_z
    coarse, every_x, every_z = (coarse, add_every_x, add_every_z)
    fine_u = high_u.reshape(points, levels)
    fine_v = high_v.reshape(points, levels)
    coarse_u = coarse[:, :levels]
    coarse_v = coarse[:, levels:]
    self_term = (coarse_u * coarse_v + fine_u.astype(jnp.float32) * fine_v).astype(jnp.bfloat16)
    cross_term = coarse_u * fine_v + fine_u * coarse_v
    cross_round = cross_term.astype(jnp.bfloat16)
    own_weight = mode_weight(low_kx, low_kz)[:, None]
    products = jnp.concatenate([self_term, cross_round], axis=1)
    serial = jnp.arange(owned_modes * groups_x * lax.axis_size("gz"), dtype=jnp.int32)
    column = serial // (owned_modes * groups_x)
    row_group = serial // owned_modes % groups_x
    modes = (row_group * groups_z + column) * owned_modes + serial % owned_modes
    table = patterns(jnp.take(every_x, modes), jnp.take(every_z, modes))
    column_part = lax.psum_scatter(
        jnp.dot(table, products, preferred_element_type=jnp.float32) * unitary,
        "gz",
        scatter_dimension=0,
        tiled=True,
    )
    totals = sent_and_summed(column_part, "gx", 0)
    forcing = totals[:, :levels]
    cross_low = (own_weight * totals[:, levels:]).astype(jnp.bfloat16)
    index_x = every_x
    index_z = every_z
    restored = lax.dot_general(
        patterns(index_x, index_z),
        lax.all_gather(cross_low, ("gx", "gz"), axis=0, tiled=True),
        CONTRACT_FIRST,
        preferred_element_type=jnp.float32,
    )
    high_term = (
        (cross_term - unitary * restored).astype(jnp.bfloat16).reshape(cells_x, cells_z, levels)
    )
    low_response = jnp.einsum(
        "mij,mj->mi", tau_inverse, forcing.astype(jnp.bfloat16), preferred_element_type=jnp.float32
    )
    return (high_term, low_response)


def solution(mesh):
    placed = (
        P("gx", "gz", None),
        P("gx", "gz", None),
        P(("gx", "gz"), None),
        P(("gx", "gz"), None),
        P(("gx", "gz")),
        P(("gx", "gz")),
        P(("gx", "gz"), None, None),
    )
    return jax.shard_map(
        on_device,
        mesh=mesh,
        in_specs=placed,
        out_specs=(P("gx", "gz", None), P(("gx", "gz"), None)),
        check_vma=False,
    )
```

profile of v0, /device:TPU:1, one launch (start us, length us, event | category | flops | bytes accessed | tf_op | source)
XLA Modules:
  0.0 554.5 jit_solution(8208175064779380195)
XLA Ops:
  7.2 0.0 all-gather.3.cloned.1.call-start
  7.2 0.7 convert_bitcast_fusion.1
  7.9 0.1 copy.11
  8.0 0.7 convert_bitcast_fusion
  8.6 0.1 copy.12
  8.7 1.4 concatenate.9
  10.2 0.0 all-gather.3.cloned.1.call-update
  10.2 0.0 reduce-scatter.2.cloned.1.call-start
  10.3 201.3 %all-gather.3.cloned.1.call-done = bf16[2048,1026]{1,0:T(8,128)(2,1)} async-done(((bf16[16,1026]{1,0:T(8,128)(2,1)}), bf16[2048,1026]{1,0:T(8,128)(2,1)}) %all-gather.3.cloned.1.call-update) | async-done | bytes 4202512 | tf_op jit(solution)/shard_map/all_gather | solution.py:14
  211.6 2.5 convert_reduce_fusion.1
  214.1 11.8 %gather_fusion.1 = s32[2048]{0:T(1024)S(1)} fusion(s32[2048]{0:T(1024)S(1)} %get-tuple-element.5, s32[2048]{0:T(1024)S(1)} %broadcast_clamp_fusion), kind=kCustom, calls=%fused_computation.1.clone | custom fusion | bytes 24576 | tf_op jit(solution)/shard_map/jit(_take)/gather | solution.py:93
  226.0 11.8 %gather_fusion = s32[2048]{0:T(1024)S(1)} fusion(s32[2048]{0:T(1024)S(1)} %get-tuple-element.3, s32[2048]{0:T(1024)S(1)} %broadcast_clamp_fusion), kind=kCustom, calls=%fused_computation.clone | custom fusion | bytes 24576 | tf_op jit(solution)/shard_map/jit(_take)/gather | solution.py:93
  237.8 2.0 fusion.8
  239.8 4.2 sine_select_fusion
  244.0 1.1 multiply_convert_fusion.1
  245.1 1.1 multiply_convert_fusion
  246.2 0.9 copy-done
  247.1 0.0 copy-start.2
  247.1 4.5 fusion
  251.6 1.1 fusion.44
  252.7 7.2 %convolution_multiply_fusion = f32[2048,1024]{1,0:T(8,128)} fusion(bf16[2048,1024]{0,1:T(8,128)(2,1)S(1)} %bitcast.30, bf16[1024,512]{1,0:T(8,128)(2,1)S(1)} %get-tuple-element.9, bf16[1024,512]{1,0:T(8,128)(2,1)S(1)} %get-tuple-element.11), kind=kOutput, calls=%fused_computation.4 | convolution fusion | flops 4301258752 | bytes 14680064 | tf_op jit(solution)/shard_map/dot_general | solution.py:95
  259.9 0.0 reduce-scatter.2.cloned.1.call-update
  260.0 69.8 %reduce-scatter.2.cloned.1.call-done = f32[128,1024]{1,0:T(8,128)} async-done(((f32[2048,1024]{1,0:T(8,128)}), f32[128,1024]{1,0:T(8,128)}) %reduce-scatter.2.cloned.1.call-update) | async-done | bytes 524304 | tf_op jit(solution)/shard_map/reduce_scatter | solution.py:94
  329.8 6.6 %all-to-all-start = ((f32[8,16,1024]{2,1,0:T(8,128)}), f32[8,16,1024]{2,1,0:T(8,128)S(1)}, u32[]{:S(2)}, u32[]{:S(2)}) async-start(f32[8,16,1024]{2,1,0:T(8,128)} %bitcast.33), calls=%async_computation.1 | async-start | bytes 1048576 | tf_op jit(solution)/shard_map/all_to_all | solution.py:30
  336.4 0.0 all-gather.5.cloned.1.call-start
  336.5 9.0 %all-to-all-done = f32[8,16,1024]{2,1,0:T(8,128)S(1)} async-done(((f32[8,16,1024]{2,1,0:T(8,128)}), f32[8,16,1024]{2,1,0:T(8,128)S(1)}, u32[]{:S(2)}, u32[]{:S(2)}) %all-to-all-start) | async-done | bytes 524320 | tf_op jit(solution)/shard_map/all_to_all | solution.py:30
  345.5 0.7 fusion.24
  346.2 0.0 all-gather.5.cloned.1.call-update
  346.2 5.6 %fusion.25 = f32[16,1,512]{2,1,0:T(1,128)S(1)} fusion(bf16[16,512,512]{2,1,0:T(8,128)(2,1)} %param.15, bf16[16,512,1]{1,0,2:T(8,128)(2,1)S(1)} %fusion.31), kind=kOutput, calls=%fused_computation.69 | convolution fusion | flops 8388608 | bytes 8437760 | tf_op jit(solution)/shard_map/mij,mj->mi/dot_general | solution.py:114
  351.8 0.6 copy.18
  352.5 189.4 %all-gather.5.cloned.1.call-done = bf16[2048,512]{1,0:T(8,128)(2,1)} async-done(((bf16[16,512]{1,0:T(8,128)(2,1)}), bf16[2048,512]{1,0:T(8,128)(2,1)}) %all-gather.5.cloned.1.call-update) | async-done | bytes 2097168 | tf_op jit(solution)/shard_map/all_gather | solution.py:107
  541.8 6.2 %subtract_convert_fusion = bf16[1024,512]{1,0:T(8,128)(2,1)} fusion(f32[1024,512]{1,0:T(8,128)S(1)} %get-tuple-element.10, bf16[2048,1024]{0,1:T(8,128)(2,1)} %bitcast.29, bf16[2048,512]{1,0:T(8,128)(2,1)} %all-gather.5.cloned.1.call-done), kind=kOutput, calls=%fused_computation.16 | convolution fusion | flops 2149056512 | bytes 9437184 | tf_op jit(solution)/shard_map/dot_general | solution.py:105
  (23 shorter events, 0.1 us)
Async XLA Ops:
  7.2 204.4 %all-gather.3.cloned.1.call-start = ((), (), s32[]{:S(2)}) async-start(), calls=%async_computation.2 | async-start | bytes 4755456 | tf_op jit(solution)/shard_map/all_gather | solution.py:14
  10.2 319.6 %reduce-scatter.2.cloned.1.call-start = ((), (), s32[]{:S(2)}) async-start(), calls=%async_computation.3 | async-start | bytes 8912896 | tf_op jit(solution)/shard_map/reduce_scatter | solution.py:94
  239.8 7.3 %slice-start = ((s8[4718592]{0:T(1024)(128)(4,1)}), s8[4194304]{0:T(1024)(128)(4,1)S(1)}, s32[]{:S(2)}) async-start(s8[4718592]{0:T(1024)(128)(4,1)} %bitcast.31), calls=%async_computation.5 | async-start | bytes 8388608
  244.0 3.1 slice-start.1
  245.1 2.0 copy-start
  247.1 4.5 copy-start.1
  247.1 4.5 copy-start.2
  259.9 76.5 %copy-start.3 = (s32[16]{0:T(128)S(1)}, s32[16]{0:T(128)}, u32[]{:S(2)}) copy-start(s32[16]{0:T(128)} %param.13) | copy-start | bytes 196
  259.9 76.5 %copy-start.4 = (s32[16]{0:T(128)S(1)}, s32[16]{0:T(128)}, u32[]{:S(2)}) copy-start(s32[16]{0:T(128)} %param.14) | copy-start | bytes 196
  329.8 15.7 %all-to-all-start = ((f32[8,16,1024]{2,1,0:T(8,128)}), f32[8,16,1024]{2,1,0:T(8,128)S(1)}, u32[]{:S(2)}, u32[]{:S(2)}) async-start(f32[8,16,1024]{2,1,0:T(8,128)} %bitcast.33), calls=%async_computation.1 | async-start | bytes 1048576 | tf_op jit(solution)/shard_map/all_to_all | solution.py:30
  336.4 205.4 %all-gather.5.cloned.1.call-start = ((), (), s32[]{:S(2)}) async-start(), calls=%async_computation.4 | async-start | bytes 2113536 | tf_op jit(solution)/shard_map/all_gather | solution.py:107
Sparse Core Ops, SparseCore 0:
  10.3 201.2 all-gather.2
  260.1 69.6 reduce-scatter.1
  346.3 195.4 all-gather.4
where the time goes:
time: 555 us
  waiting for transfers between devices  470 us (85%)
  local copies, waits for them, and re-layouts  26.7 us (5%)
  matrix products  23.5 us (4%)
  other arithmetic  14.1 us (3%)
  between operations  13.9 us (3%)
  starting transfers between devices  6.72 us (1%)
    all_gather x1, waiting for transfers between devices, in_one_piece(): whole, at, done = (lax.all_gather(both, axis, axis=dim, tiled=True), 0, [])  201 us
    all_gather x1, waiting for transfers between devices, on_device(): lax.all_gather(cross_low, ('gx', 'gz'), axis=0, tiled=True)  189 us
    reduce_scatter x1, waiting for transfers between devices, on_device(): lax.psum_scatter(jnp.dot(table, products, preferred_element_type=jnp.floa...  69.8 us
    gather x2, local copies, waits for them, and re-layouts, on_device(): table = patterns(jnp.take(every_x, modes), jnp.take(every_z, modes))  23.6 us
  transfers between devices with their start and end apart: 4, of which 4 were waited for; matrix products, arithmetic and copies ran while one was open for 1% of the time, Pallas kernels for 0%

commit v1 on v0

--- a/solution.py
+++ b/solution.py
@@ -6,6 +6,11 @@
 
 KL = 32
 CONTRACT_FIRST = (((0,), (0,)), ((), ()))
+
+
+def gather_over(x, axis, dim):
+    sent = jnp.stack([x] * lax.axis_size(axis))
+    return jnp.concatenate(lax.all_to_all(sent, axis, 0, 0), axis=dim)
 
 
 def in_one_piece(arrays, axis, dim, along):
@@ -104,7 +109,7 @@
     index_z = every_z
     restored = lax.dot_general(
         patterns(index_x, index_z),
-        lax.all_gather(cross_low, ("gx", "gz"), axis=0, tiled=True),
+        gather_over(cross_low, ("gx", "gz"), 0),
         CONTRACT_FIRST,
         preferred_element_type=jnp.float32,
     )

time: 555 us -> 401 us (0.72)
  waiting for transfers between devices: 470 us -> 304 us
  starting transfers between devices: 6.72 us -> 16.8 us
    all_gather x1 -> x0, waiting for transfers between devices: 189 us -> none  [on_device(): lax.all_gather(cross_low, ('gx', 'gz'), axis=0, tiled=True)]
    all_to_all x0 -> x1, waiting for transfers between devices: none -> 24.2 us  [gather_over(): return jnp.concatenate(lax.all_to_all(sent, axis, 0, 0), axis=dim)]
    all_to_all x0 -> x1, starting transfers between devices: none -> 10.3 us  [gather_over(): return jnp.concatenate(lax.all_to_all(sent, axis, 0, 0), axis=dim)]
  transfers between devices with their start and end apart: 4 -> 4, of which waited for: 4 -> 4; matrix products, arithmetic and copies ran while one was open for 1% -> 2% of each run, Pallas kernels for 0% -> 0%
where the time goes in v1:
time: 401 us
  waiting for transfers between devices  304 us (76%)
  local copies, waits for them, and re-layouts  28.3 us (7%)
  matrix products  23.6 us (6%)
  starting transfers between devices  16.8 us (4%)
  between operations  14.2 us (4%)
  other arithmetic  13.6 us (3%)
    all_gather x1, waiting for transfers between devices, in_one_piece(): whole, at, done = (lax.all_gather(both, axis, axis=dim, tiled=True), 0, [])  201 us
    reduce_scatter x1, waiting for transfers between devices, on_device(): lax.psum_scatter(jnp.dot(table, products, preferred_element_type=jnp.floa...  70 us
    all_to_all x1, waiting for transfers between devices, gather_over(): return jnp.concatenate(lax.all_to_all(sent, axis, 0, 0), axis=dim)  24.2 us
    gather x2, local copies, waits for them, and re-layouts, on_device(): table = patterns(jnp.take(every_x, modes), jnp.take(every_z, modes))  23.6 us
    all_to_all x1, starting transfers between devices, gather_over(): return jnp.concatenate(lax.all_to_all(sent, axis, 0, 0), axis=dim)  10.3 us
    all_to_all x1, waiting for transfers between devices, sent_and_summed(): pieces = lax.all_to_all(cut_along(x, dim, count), axis, 0, 0, tiled=True)  9.02 us
  transfers between devices with their start and end apart: 4, of which 4 were waited for; matrix products, arithmetic and copies ran while one was open for 2% of the time, Pallas kernels for 0%

profile of v1, /device:TPU:1, one launch (start us, length us, event | category | flops | bytes accessed | tf_op | source)
XLA Modules:
  0.0 400.9 jit_solution(1818045036313394778)
XLA Ops:
  7.2 0.0 all-gather.2.cloned.1.call-start
  7.2 0.7 convert_bitcast_fusion.1
  7.9 0.1 copy.11
  8.0 0.7 convert_bitcast_fusion
  8.6 0.1 copy.12
  8.7 1.4 concatenate.9
  10.2 0.0 all-gather.2.cloned.1.call-update
  10.2 0.0 reduce-scatter.2.cloned.1.call-start
  10.3 201.2 %all-gather.2.cloned.1.call-done = bf16[2048,1026]{1,0:T(8,128)(2,1)} async-done(((bf16[16,1026]{1,0:T(8,128)(2,1)}), bf16[2048,1026]{1,0:T(8,128)(2,1)}) %all-gather.2.cloned.1.call-update) | async-done | bytes 4202512 | tf_op jit(solution)/shard_map/all_gather | solution.py:19
  211.4 2.6 convert_reduce_fusion.1
  214.0 11.8 %gather_fusion.1 = s32[2048]{0:T(1024)S(1)} fusion(s32[2048]{0:T(1024)S(1)} %get-tuple-element.5, s32[2048]{0:T(1024)S(1)} %broadcast_clamp_fusion), kind=kCustom, calls=%fused_computation.1.clone | custom fusion | bytes 24576 | tf_op jit(solution)/shard_map/jit(_take)/gather | solution.py:98
  225.9 11.8 %gather_fusion = s32[2048]{0:T(1024)S(1)} fusion(s32[2048]{0:T(1024)S(1)} %get-tuple-element.3, s32[2048]{0:T(1024)S(1)} %broadcast_clamp_fusion), kind=kCustom, calls=%fused_computation.clone | custom fusion | bytes 24576 | tf_op jit(solution)/shard_map/jit(_take)/gather | solution.py:98
  237.7 2.1 fusion.8
  239.8 4.2 %sine_select_fusion = (f32[2048,32]{0,1:T(8,128)S(1)}, f32[2048,32]{0,1:T(8,128)S(1)}, f32[2048,32]{0,1:T(8,128)S(1)}, f32[2048,32]{0,1:T(8,128)S(1)}) fusion(s32[2048]{0:T(1024)S(1)} %add_select_fusion.4, s32[32]{0:T(128)S(1)} %iota_add_fusion, pred[2048]{0:T(1024)(128)(4,1)S(1)} %select_compare_fusion, s32[2048]{0:T(1024)S(1)} %get-tuple-element.6, ...), kind=kLoop, calls=%fused_computation.61 | loop fusion | flops 3932160 | bytes 1089792 | tf_op jit(solution)/shard_map/jit(_where)/select_n | solution.py:43
  244.0 1.1 multiply_convert_fusion.1
  245.1 1.1 multiply_convert_fusion
  246.2 0.9 copy-done
  247.0 0.0 copy-start.2
  247.1 4.5 %fusion = f32[1024,1024]{1,0:T(8,128)S(1)} fusion(bf16[2048,1024]{0,1:T(8,128)(2,1)S(1)} %bitcast.29, bf16[2048,1026]{1,0:T(8,128)(2,1)S(1)} %bitcast.33), kind=kOutput, calls=%fused_computation.5 | convolution fusion | flops 4294967296 | bytes 12582912 | tf_op jit(solution)/shard_map/dot_general | solution.py:79
  251.6 1.1 fusion.44
  252.6 7.3 %convolution_multiply_fusion = f32[2048,1024]{1,0:T(8,128)} fusion(bf16[2048,1024]{0,1:T(8,128)(2,1)S(1)} %bitcast.31, bf16[1024,512]{1,0:T(8,128)(2,1)S(1)} %get-tuple-element.9, bf16[1024,512]{1,0:T(8,128)(2,1)S(1)} %get-tuple-element.11), kind=kOutput, calls=%fused_computation.4 | convolution fusion | flops 4301258752 | bytes 14680064 | tf_op jit(solution)/shard_map/dot_general | solution.py:100
  259.9 0.0 reduce-scatter.2.cloned.1.call-update
  260.0 70.0 %reduce-scatter.2.cloned.1.call-done = f32[128,1024]{1,0:T(8,128)} async-done(((f32[2048,1024]{1,0:T(8,128)}), f32[128,1024]{1,0:T(8,128)}) %reduce-scatter.2.cloned.1.call-update) | async-done | bytes 524304 | tf_op jit(solution)/shard_map/reduce_scatter | solution.py:99
  330.0 6.4 %all-to-all-start = ((f32[8,16,1024]{2,1,0:T(8,128)}), f32[8,16,1024]{2,1,0:T(8,128)S(1)}, u32[]{:S(2)}, u32[]{:S(2)}) async-start(f32[8,16,1024]{2,1,0:T(8,128)} %bitcast.34), calls=%async_computation.1 | async-start | bytes 1048576 | tf_op jit(solution)/shard_map/all_to_all | solution.py:35
  336.4 9.0 %all-to-all-done = f32[8,16,1024]{2,1,0:T(8,128)S(1)} async-done(((f32[8,16,1024]{2,1,0:T(8,128)}), f32[8,16,1024]{2,1,0:T(8,128)S(1)}, u32[]{:S(2)}, u32[]{:S(2)}) %all-to-all-start) | async-done | bytes 524320 | tf_op jit(solution)/shard_map/all_to_all | solution.py:35
  345.5 0.1 fusion.24
  345.5 1.6 stack.2
  347.1 10.3 %all-to-all-start.1 = ((bf16[128,16,512]{2,1,0:T(8,128)(2,1)}), bf16[128,16,512]{2,1,0:T(8,128)(2,1)}, u32[]{:S(2)}, u32[]{:S(2)}) async-start(bf16[128,16,512]{2,1,0:T(8,128)(2,1)} %stack.2), calls=%async_computation.2 | async-start | bytes 4194304 | tf_op jit(solution)/shard_map/all_to_all | solution.py:13
  357.4 5.6 %fusion.25 = f32[16,1,512]{2,1,0:T(1,128)S(1)} fusion(bf16[16,512,512]{2,1,0:T(8,128)(2,1)} %param.15, bf16[16,512,1]{1,0,2:T(8,128)(2,1)S(1)} %fusion.31), kind=kOutput, calls=%fused_computation.69 | convolution fusion | flops 8388608 | bytes 8437760 | tf_op jit(solution)/shard_map/mij,mj->mi/dot_general | solution.py:119
  363.0 0.6 copy.18
  363.7 24.2 %all-to-all-done.1 = bf16[128,16,512]{2,1,0:T(8,128)(2,1)} async-done(((bf16[128,16,512]{2,1,0:T(8,128)(2,1)}), bf16[128,16,512]{2,1,0:T(8,128)(2,1)}, u32[]{:S(2)}, u32[]{:S(2)}) %all-to-all-start.1) | async-done | bytes 2097184 | tf_op jit(solution)/shard_map/all_to_all | solution.py:13
  387.9 6.2 %subtract_convert_fusion = bf16[1024,512]{1,0:T(8,128)(2,1)} fusion(f32[1024,512]{1,0:T(8,128)S(1)} %get-tuple-element.10, bf16[2048,1024]{0,1:T(8,128)(2,1)} %bitcast.30, bf16[2048,512]{1,0:T(8,128)(2,1)} %bitcast.9), kind=kOutput, calls=%fused_computation.16 | convolution fusion | flops 2149056512 | bytes 9437184 | tf_op jit(solution)/shard_map/dot_general | solution.py:110
  (23 shorter events, 0.1 us)
Async XLA Ops:
  7.2 204.3 %all-gather.2.cloned.1.call-start = ((), (), s32[]{:S(2)}) async-start(), calls=%async_computation.3 | async-start | bytes 4755456 | tf_op jit(solution)/shard_map/all_gather | solution.py:19
  10.2 319.8 %reduce-scatter.2.cloned.1.call-start = ((), (), s32[]{:S(2)}) async-start(), calls=%async_computation.4 | async-start | bytes 8912896 | tf_op jit(solution)/shard_map/reduce_scatter | solution.py:99
  239.8 7.3 %slice-start = ((s8[4718592]{0:T(1024)(128)(4,1)}), s8[4194304]{0:T(1024)(128)(4,1)S(1)}, s32[]{:S(2)}) async-start(s8[4718592]{0:T(1024)(128)(4,1)} %bitcast.32), calls=%async_computation.5 | async-start | bytes 8388608
  244.0 3.1 slice-start.1
  245.1 2.0 copy-start
  247.0 4.5 %copy-start.1 = (bf16[32,32,512]{2,1,0:T(8,128)(2,1)S(1)}, bf16[32,32,512]{2,1,0:T(8,128)(2,1)}, u32[]{:S(2)}) copy-start(bf16[32,32,512]{2,1,0:T(8,128)(2,1)} %param.9) | copy-start | bytes 3145732
  247.0 4.5 %copy-start.2 = (bf16[32,32,512]{2,1,0:T(8,128)(2,1)S(1)}, bf16[32,32,512]{2,1,0:T(8,128)(2,1)}, u32[]{:S(2)}) copy-start(bf16[32,32,512]{2,1,0:T(8,128)(2,1)} %param.10) | copy-start | bytes 3145732
  259.9 76.5 %copy-start.3 = (s32[16]{0:T(128)S(1)}, s32[16]{0:T(128)}, u32[]{:S(2)}) copy-start(s32[16]{0:T(128)} %param.13) | copy-start | bytes 196
  259.9 76.5 %copy-start.4 = (s32[16]{0:T(128)S(1)}, s32[16]{0:T(128)}, u32[]{:S(2)}) copy-start(s32[16]{0:T(128)} %param.14) | copy-start | bytes 196
  330.0 15.5 %all-to-all-start = ((f32[8,16,1024]{2,1,0:T(8,128)}), f32[8,16,1024]{2,1,0:T(8,128)S(1)}, u32[]{:S(2)}, u32[]{:S(2)}) async-start(f32[8,16,1024]{2,1,0:T(8,128)} %bitcast.34), calls=%async_computation.1 | async-start | bytes 1048576 | tf_op jit(solution)/shard_map/all_to_all | solution.py:35
  347.1 40.8 %all-to-all-start.1 = ((bf16[128,16,512]{2,1,0:T(8,128)(2,1)}), bf16[128,16,512]{2,1,0:T(8,128)(2,1)}, u32[]{:S(2)}, u32[]{:S(2)}) async-start(bf16[128,16,512]{2,1,0:T(8,128)(2,1)} %stack.2), calls=%async_computation.2 | async-start | bytes 4194304 | tf_op jit(solution)/shard_map/all_to_all | solution.py:13
Sparse Core Ops, SparseCore 0:
  10.3 201.0 all-gather.1
  260.1 69.8 reduce-scatter.1
